TPU v7x, 32 devices: a whole 2x2x4 slice. The times are simulated.
32 devices in a mesh: vocab: 8 (over z, y), layer: 4 (over x, core).
Axes of the slice: x: 2, y: 2, z: 4, core: 2. Of those that a mesh axis runs over, the one named last changes fastest.
Arguments:
- residual: bfloat16 [1024, 8192], P('layer', 'vocab'), may hold values from -40 to 40
- gain: bfloat16 [1, 8192], P(None, 'vocab'), may hold values from 0.25 to 1.75
- unembed: bfloat16 [8192, 128256], P(None, ('vocab', 'layer')), may hold values from -0.22097087 to 0.22097087
Outputs:
- log_probs: float32 [1024, 128256], P('layer', 'vocab')
All inputs are finite; a program needn't handle non-finite values.
Results may differ from a plain program's by a relative error of at most 0.0003.
Values may be sent and summed in bfloat16 or wider, within the bound.
No kernel may reach another device: no remote copies, remote signals or barrier semaphores. Data moves between devices by JAX's collectives and lax.ppermute only.
A program may use at most 192 MiB of HBM per device.

v0:
```python
import jax
import jax.numpy as jnp
from jax import lax
from jax.sharding import PartitionSpec as P

D = 8192


def joined(shard, axis, combine):
    everything = jax.tree.map(lambda part: lax.all_gather(part, axis), shard)
    initial = jax.tree.map(lambda part: part[0], everything)

    def lap(k, so_far):
        return combine(so_far, jax.tree.map(lambda part: part[k], everything))

    return lax.fori_loop(1, lax.axis_size(axis), lap, initial)


def combine_pairs(earlier, later):
    highest = jnp.maximum(earlier[0], later[0])
    totals = earlier[1] * jnp.exp(earlier[0] - highest) + later[1] * jnp.exp(later[0] - highest)
    return (highest, totals)


def local(residual, gain, unembed):
    full_rows, full_gain = (
        lax.all_gather(residual, "vocab", axis=1, tiled=True),
        lax.all_gather(gain, "vocab", axis=1, tiled=True),
    )
    all_rows = lax.all_gather(full_rows, "layer", axis=0, tiled=True)
    widened = all_rows.astype(jnp.float32)
    squares = jnp.sum(widened * widened, axis=1)
    scaled = (widened * full_gain.astype(jnp.float32)).astype(jnp.bfloat16)
    products = jnp.dot(scaled, unembed, preferred_element_type=jnp.float32)
    inverse = lax.rsqrt(squares / D + 1e-05)
    logits = products * inverse[:, None]
    local_max = jnp.max(logits, axis=1)
    local_sums = jnp.sum(jnp.exp(logits - local_max[:, None]), axis=1)
    highest, totals = joined((local_max, local_sums), ("vocab", "layer"), combine_pairs)
    lse = highest + jnp.log(totals)
    log_values = logits - lse[:, None]
    return lax.all_to_all(log_values, "layer", split_axis=0, concat_axis=1, tiled=True)


def solution(mesh):
    placed = (P("layer", "vocab"), P(None, "vocab"), P(None, ("vocab", "layer")))
    return jax.shard_map(
        local, mesh=mesh, in_specs=placed, out_specs=P("layer", "vocab"), check_vma=False
    )
```

profile of v0, /device:TPU:0, one launch (start us, length us, event | category | flops | bytes accessed | tf_op | source)
XLA Modules:
  0.0 570.1 jit_solution(13721698906693469134)
XLA Ops:
  6.5 0.0 all-gather.5.cloned.1.call-start
  6.5 0.7 all-gather.5.cloned.1.call-update
  7.3 0.0 all-gather.7.cloned.1.call-start
  7.3 77.7 %all-gather.5.cloned.1.call-done = bf16[256,8192]{1,0:T(8,128)(2,1)} async-done(((bf16[256,1024]{1,0:T(8,128)(2,1)}), bf16[256,8192]{1,0:T(8,128)(2,1)}) %all-gather.5.cloned.1.call-update) | async-done | bytes 4194320 | tf_op jit(solution)/shard_map/all_gather | solution.py:27
  85.0 0.0 all-gather.7.cloned.1.call-update
  85.1 30.7 %all_gather.23 = bf16[1,8192]{1,0:T(2,128)(2,1)S(1)} all-gather(bf16[1,1024]{1,0:T(2,128)(2,1)} %param.6), channel_id=1, replica_groups=mesh['vocab'=8,'layer'=4] {'vocab'}, dimensions={1}, use_global_device_ids=true | all-gather | bytes 18432 | tf_op jit(solution)/shard_map/all_gather | solution.py:28
  115.9 75.2 %all-gather.7.cloned.1.call-done = bf16[1024,8192]{1,0:T(8,128)(2,1)} async-done(((bf16[256,8192]{1,0:T(8,128)(2,1)}), bf16[1024,8192]{1,0:T(8,128)(2,1)}) %all-gather.7.cloned.1.call-update) | async-done | bytes 16777232 | tf_op jit(solution)/shard_map/all_gather | solution.py:30
  191.1 7.2 %fusion.1 = f32[1024]{0:T(1024)S(1)} fusion(bf16[1024,8192]{1,0:T(8,128)(2,1)} %all-gather.7.cloned.1.call-done), kind=kLoop, calls=%fused_computation.6 | loop fusion | flops 25164800 | bytes 16781312 | tf_op jit(solution)/shard_map/reduce_sum | solution.py:32
  198.3 79.6 %multiply_reduce_fusion = (f32[1024]{0:T(1024)S(1)}, f32[1024,4008]{0,1:T(8,128)}) fusion(f32[1024]{0:T(1024)S(1)} %add_rsqrt_fusion, bf16[8192,4008]{0,1:T(8,128)(2,1)} %param.7, bf16[1024,8192]{1,0:T(8,128)(2,1)} %all-gather.7.cloned.1.call-done, f32[8192]{0:T(1024)S(1)} %bitcast.21), kind=kOutput, calls=%fused_computation.12 | convolution fusion | flops 67276455936 | bytes 98902016 | tf_op jit(solution)/shard_map/dot_general | solution.py:34
  277.9 8.4 %exponential_reduce_fusion = f32[1024]{0:T(1024)S(1)} fusion(f32[1024,4008]{0,1:T(8,128)} %get-tuple-element.155, f32[1024]{0:T(1024)S(1)} %get-tuple-element.154, f32[1024]{0:T(1024)S(1)} %add_rsqrt_fusion), kind=kLoop, calls=%fused_computation.10 | loop fusion | flops 12311552 | bytes 16429056 | tf_op jit(solution)/shard_map/reduce_sum | solution.py:38
  286.3 40.9 %all-gather.1 = f32[32768]{0:T(1024)S(1)} all-gather(f32[1024]{0:T(1024)S(1)} %exponential_reduce_fusion), channel_id=3, replica_groups=mesh['vocab'=8,'layer'=4] {'vocab','layer'}, dimensions={0}, use_global_device_ids=true | all-gather | bytes 135168 | tf_op jit(solution)/shard_map/all_gather | solution.py:10
  327.2 37.0 %all-gather = f32[32768]{0:T(1024)S(1)} all-gather(f32[1024]{0:T(1024)S(1)} %get-tuple-element.154), channel_id=2, replica_groups=mesh['vocab'=8,'layer'=4] {'vocab','layer'}, dimensions={0}, use_global_device_ids=true | all-gather | bytes 135168 | tf_op jit(solution)/shard_map/all_gather | solution.py:10
  364.2 1.8 while.17
  366.1 7.2 %multiply_subtract_fusion = f32[1024,4008]{0,1:T(8,128)S(1)} fusion(f32[1024,4008]{0,1:T(8,128)} %get-tuple-element.155, f32[1024]{0:T(1024)S(1)} %log_add_fusion, f32[1024]{0:T(1024)S(1)} %add_rsqrt_fusion), kind=kLoop, calls=%fused_computation.11 | loop fusion | flops 8208384 | bytes 32841728 | tf_op jit(solution)/shard_map/sub | solution.py:41
  373.3 1.8 copy.8
  375.1 182.2 %all_to_all.19 = f32[4,256,4008]{1,2,0:T(8,128)S(1)} all-to-all(f32[4,256,4008]{1,2,0:T(8,128)S(1)} %bitcast.17), channel_id=1, replica_groups=mesh['vocab'=8,'layer'=4] {'layer'}, dimensions={0} | all-to-all | bytes 32833536 | tf_op jit(solution)/shard_map/all_to_all | solution.py:42
  557.3 6.0 %copy.19 = f32[256,16032]{0,1:T(8,128)} copy(f32[256,16032]{0,1:T(8,128)S(1)} %bitcast.18) | data formatting | bytes 32833536
  (69 shorter events, 0.9 us)
Async XLA Ops:
  6.5 78.5 %all-gather.5.cloned.1.call-start = ((), (), s32[]{:S(2)}) async-start(), calls=%async_computation.1 | async-start | bytes 4718592 | tf_op jit(solution)/shard_map/all_gather | solution.py:27
  7.3 183.8 %all-gather.7.cloned.1.call-start = ((), (), s32[]{:S(2)}) async-start(), calls=%async_computation.2 | async-start | bytes 20971520 | tf_op jit(solution)/shard_map/all_gather | solution.py:30
Sparse Core Ops, SparseCore 0:
  9.5 75.4 all-gather.4
  86.6 104.4 all-gather.6
where the time goes:
time: 570 us
  blocking collectives  291 us (51%)
  waiting for transfers between devices  154 us (27%)
  matrix products  79.6 us (14%)
  other arithmetic  23.2 us (4%)
  between operations  13.5 us (2%)
  local copies, waits for them, and re-layouts  8.36 us (1%)
    all_to_all x1, blocking collectives, local(): lax.all_to_all(log_values, 'layer', split_axis=0, concat_axis=1, tiled=True)  182 us
    dot_general x1, matrix products, local(): products = jnp.dot(scaled, unembed, preferred_element_type=jnp.float32)  79.6 us
    all_gather x2, blocking collectives, joined(): everything = jax.tree.map(lambda part: lax.all_gather(part, axis), shard)  77.9 us
    all_gather x1, waiting for transfers between devices, local(): lax.all_gather(residual, 'vocab', axis=1, tiled=True)  77.7 us
    all_gather x1, waiting for transfers between devices, local(): all_rows = lax.all_gather(full_rows, 'layer', axis=0, tiled=True)  75.2 us
    all_gather x1, blocking collectives, local(): lax.all_gather(gain, 'vocab', axis=1, tiled=True)  30.7 us
  transfers between devices with their start and end apart: 2, of which 2 were waited for; matrix products, arithmetic and copies ran while one was open for 0% of the time, Pallas kernels for 0%

commit v1 on v0

v1 whole, which is shorter than its diff:
```python
import functools

import jax
import jax.numpy as jnp
from jax import lax
from jax.experimental import pallas as pl
from jax.experimental.pallas import tpu as pltpu
from jax.sharding import PartitionSpec as P


EPS = 1e-05
TILE = 512
CHUNK = 1024
FIRST, LATER = 1024, 1536
DEPTH = 4
SPAN = 250.0
LN2 = 0.6931471805599453
AXES = ("vocab", "layer")
F32 = jnp.float32
BF16 = jnp.bfloat16
VMEM_LIMIT = 28 * 1024 * 1024
JOIN_LIMIT = 12 * 1024 * 1024
NT = (((1,), (1,)), ((), ()))
HBM = pl.BlockSpec(memory_space=pl.ANY)
VMEM = pl.BlockSpec(memory_space=pltpu.VMEM)


def sum_slots(rows, width):
    piece = min(rows, width)
    per_tile = width // piece
    slots = []
    for q in range(3 * (rows // piece)):
        slots.append((q // (rows // piece), (q % (rows // piece)) * piece, 16 * (q // per_tile), (q % per_tile) * piece))
    return piece, slots, 16 * (slots[-1][2] // 16 + 1)


def pack_kernel(residual_ref, gain_ref, out_ref):
    rows, width = residual_ref.shape
    piece, slots, _ = sum_slots(rows, width)
    wide = residual_ref[...].astype(F32)
    out_ref[pl.ds(0, rows), :] = (wide * gain_ref[...].astype(F32)).astype(BF16)
    square = wide * wide
    high = square.astype(BF16)
    low = (square - high.astype(F32)).astype(BF16)
    ones = jnp.ones((16, width), BF16)
    sums = lax.dot_general(ones, high, NT, preferred_element_type=F32)
    sums = sums + lax.dot_general(ones, low, NT, preferred_element_type=F32)
    parts = []
    for _ in range(3):
        part = sums.astype(BF16)
        sums = sums - part.astype(F32)
        parts.append(part)
    out_ref[pl.ds(rows, out_ref.shape[0] - rows), :] = jnp.zeros((out_ref.shape[0] - rows, width), BF16)
    for part, first, row, lane in slots:
        out_ref[pl.ds(rows + row, 16), pl.ds(lane, piece)] = parts[part][:, first : first + piece]


def pack(residual, gain):
    rows, width = residual.shape
    extra = sum_slots(rows, width)[2]
    return pl.pallas_call(
        pack_kernel,
        out_shape=jax.ShapeDtypeStruct((rows + extra, width), BF16),
        in_specs=[VMEM, VMEM],
        out_specs=VMEM,
    )(residual, gain)


def join_kernel(n_groups, stacks, indices, rows, *refs):
    n = len(stacks)
    block_refs = refs[: n * n_groups]
    a_ref, inverse_ref, sums_ref, sem = refs[n * n_groups + 1 :]
    width = block_refs[0].shape[2]
    piece, slots, extra = sum_slots(rows, width)
    vocab = lax.axis_index("vocab")
    copies = []
    for g in range(n_groups):
        slot = 0
        for j in range(n):
            ref = block_refs[g * n + j]
            for k in range(stacks[j]):
                at = pl.multiple_of(indices[j](vocab, k) * width, width)
                copies.append(pltpu.make_async_copy(ref.at[k, pl.ds(0, rows), :], a_ref.at[pl.ds(g * rows, rows), pl.ds(at, width)], sem))
                copies.append(pltpu.make_async_copy(ref.at[k, pl.ds(rows, extra), :], sums_ref.at[g, slot], sem))
                slot += 1
    for copy in copies:
        copy.start()
    for copy in copies:
        copy.wait()
    for g in range(n_groups):
        for row_first in range(0, rows, piece):
            total = jnp.zeros((16, piece), F32)
            for part, at, row, lane in slots:
                if at == row_first:
                    total = total + jnp.sum(sums_ref[g, :, pl.ds(row, 16), pl.ds(lane, piece)].astype(F32), axis=0)
            features = width * sum(stacks)
            inverse = lax.rsqrt(total / features + EPS)
            inverse_ref[:, pl.ds(g * rows + row_first, piece)] = inverse[0:8, :]


def join(groups, indices, rows, after):
    stacks = [block.shape[0] for block in groups[0]]
    width = groups[0][0].shape[2]
    extra, features = sum_slots(rows, width)[2], width * sum(stacks)
    total = rows * len(groups)
    return pl.pallas_call(
        functools.partial(join_kernel, len(groups), stacks, indices, rows),
        out_shape=[jax.ShapeDtypeStruct((total, features), BF16), jax.ShapeDtypeStruct((8, total), F32)],
        in_specs=[HBM] * (len(stacks) * len(groups) + 1),
        out_specs=[VMEM, VMEM],
        scratch_shapes=[pltpu.VMEM((len(groups), sum(stacks), extra, width), BF16), pltpu.SemaphoreType.DMA],
        compiler_params=pltpu.CompilerParams(vmem_limit_bytes=JOIN_LIMIT),
        cost_estimate=pl.CostEstimate(flops=total * features, bytes_accessed=4 * total * features, transcendentals=0),
    )(*[block for group in groups for block in group], after)


def logits_kernel(n_groups, rows, columns, first, partial, w_ref, a_ref, inverse_ref, after_ref, *outs):
    del after_ref
    code_refs, stat_refs = outs[:n_groups], outs[n_groups:]
    step = pl.program_id(0)
    products = lax.dot_general(w_ref[...], a_ref[...], NT, preferred_element_type=F32)
    logits = products * inverse_ref[0:1, :]
    if partial:
        entry = first + step * TILE + lax.broadcasted_iota(jnp.int32, logits.shape, 0)
        valid = entry < columns
        logits = jnp.where(valid, logits, logits[0:1, :])
    high = jnp.max(logits, axis=0, keepdims=True)
    low = jnp.min(logits, axis=0, keepdims=True)
    scale = SPAN / jnp.maximum(high - low, 1e-6)
    codes = jnp.exp2((logits - (high + low) * 0.5) * scale).astype(BF16)
    powers = jnp.exp(logits - high)
    if partial:
        powers = jnp.where(valid, powers, 0.0)
    total = jnp.sum(powers, axis=0, keepdims=True)
    stats = jnp.concatenate([high, low, total] + [jnp.zeros_like(high)] * 5, axis=0)
    for g in range(n_groups):
        code_refs[g][...] = codes[:, g * rows : (g + 1) * rows]
        stat_refs[g][...] = stats[:, g * rows : (g + 1) * rows]


def logits_call(weights, joined, after, rows, first, count):
    scaled, inverse = joined
    columns, features = weights.shape
    n_groups, tiles = scaled.shape[0] // rows, pl.cdiv(count, TILE)
    base = first // TILE
    out = pl.pallas_call(
        functools.partial(logits_kernel, n_groups, rows, columns, first, count % TILE != 0),
        grid=(tiles,),
        in_specs=[pl.BlockSpec((TILE, features), lambda i: (base + i, 0)), VMEM, VMEM, HBM],
        out_specs=[pl.BlockSpec((TILE, rows), lambda i: (i, 0))] * n_groups + [pl.BlockSpec((8, rows), lambda i: (i, 0))] * n_groups,
        out_shape=[jax.ShapeDtypeStruct((count, rows), BF16)] * n_groups + [jax.ShapeDtypeStruct((8 * tiles, rows), F32)] * n_groups,
        compiler_params=pltpu.CompilerParams(vmem_limit_bytes=VMEM_LIMIT),
        cost_estimate=pl.CostEstimate(
            flops=2 * count * features * rows * n_groups,
            bytes_accessed=2 * count * features + 2 * rows * n_groups * features,
            transcendentals=2 * count * rows * n_groups,
        ),
    )(weights, scaled, inverse, after)
    return out[:n_groups], out[n_groups:]


def combine_kernel(*refs):
    *stat_refs, out_ref = refs
    tiles = [ref[pl.ds(8 * i, 8), :] for ref in stat_refs for i in range(ref.shape[0] // 8)]
    highest = functools.reduce(jnp.maximum, [tile[0:1, :] for tile in tiles])
    total = sum(tile[2:3, :] * jnp.exp(tile[0:1, :] - highest) for tile in tiles)
    out_ref[...] = jnp.concatenate([highest, highest, total] + [jnp.zeros_like(total)] * 5, axis=0)


def combine(stats):
    return pl.pallas_call(
        combine_kernel,
        out_shape=jax.ShapeDtypeStruct((8, stats[0].shape[1]), F32),
        in_specs=[VMEM] * len(stats),
        out_specs=VMEM,
    )(*stats)


def row_lse(totals_refs):
    pairs = [ref[pl.ds(8 * i, 8), :] for ref in totals_refs for i in range(ref.shape[0] // 8)]
    highest = functools.reduce(jnp.maximum, [pair[0:1, :] for pair in pairs])
    total = sum(pair[2:3, :] * jnp.exp(pair[0:1, :] - highest) for pair in pairs)
    return highest + jnp.log(total)


def decode_terms(stats, tile, lse):
    high, low = stats[8 * tile : 8 * tile + 1, :], stats[8 * tile + 1 : 8 * tile + 2, :]
    factor = jnp.maximum(high - low, 1e-6) * (1.0 / (SPAN * LN2))
    return factor, (high + low) * 0.5 - lse


def write_kernel(items, n_stats, n_totals, has_previous, columns, *refs):
    n_codes = 1 + max(item[4] for item in items)
    code_refs = refs[:n_codes]
    stat_refs = refs[n_codes : n_codes + n_stats]
    totals_refs = refs[n_codes + n_stats : n_codes + n_stats + n_totals]
    rest = refs[n_codes + n_stats + n_totals + has_previous :]
    out_ref, in_buf, out_buf, in_sem, out_sem = rest
    lse = row_lse(totals_refs)
    layer = lax.axis_index("layer")
    depth = DEPTH

    def fetch(i):
        count, ref, at = items[i][0], items[i][4], items[i][5]
        return pltpu.make_async_copy(code_refs[ref].at[pl.ds(at, count), :], in_buf.at[i % depth, pl.ds(0, count), :], in_sem.at[i % depth])

    def put(i):
        count, first, distance = items[i][:3]
        at = pl.multiple_of((layer ^ distance) * columns + first, 8)
        return pltpu.make_async_copy(out_buf.at[i % depth, pl.ds(0, count), :], out_ref.at[pl.ds(at, count), :], out_sem.at[i % depth])

    for i in range(min(depth, len(items))):
        fetch(i).start()
    for i, (count, first, distance, source, _, _) in enumerate(items):
        fetch(i).wait()
        if i >= depth:
            put(i - depth).wait()
        for at in range(0, count, TILE):
            size = min(TILE, count - at)
            factor, shift = decode_terms(stat_refs[source], (first + at) // TILE, lse)
            codes = in_buf[i % depth, pl.ds(at, size), :].astype(F32)
            out_buf[i % depth, pl.ds(at, size), :] = jnp.log(codes) * factor + shift
        put(i).start()
        if i + depth < len(items):
            fetch(i + depth).start()
    for i in range(max(0, len(items) - depth), len(items)):
        put(i).wait()


def write(codes, items, stats, totals, previous, columns, out_rows):
    rows = codes[0].shape[1]
    size = max(item[0] for item in items)
    n_in = len(codes) + len(stats) + len(totals)
    return pl.pallas_call(
        functools.partial(write_kernel, items, len(stats), len(totals), int(previous is not None), columns),
        out_shape=jax.ShapeDtypeStruct((out_rows, rows), F32),
        in_specs=[HBM] * len(codes) + [VMEM] * (len(stats) + len(totals)) + [HBM] * int(previous is not None),
        out_specs=HBM,
        scratch_shapes=[
            pltpu.VMEM((DEPTH, size, rows), BF16),
            pltpu.VMEM((DEPTH, size, rows), F32),
            pltpu.SemaphoreType.DMA((DEPTH,)),
            pltpu.SemaphoreType.DMA((DEPTH,)),
        ],
        input_output_aliases={n_in: 0} if previous is not None else {},
        cost_estimate=pl.CostEstimate(flops=0, bytes_accessed=6 * rows * sum(item[0] for item in items), transcendentals=0),
    )(*codes, *stats, *totals, *([previous] if previous is not None else []))


def chunks_of(columns):
    edges = [0] + list(range(FIRST, columns, LATER)) + [columns]
    return [(first, last - first) for first, last in zip(edges, edges[1:])]


def local(n_vocab, n_layer, residual, gain, unembed):
    rows = residual.shape[0]
    weights = unembed.T
    columns = weights.shape[0]

    def permute(x, move):
        pairs = []
        for v in range(n_vocab):
            for l in range(n_layer):
                to_v, to_l = move(v, l)
                pairs.append((v * n_layer + l, to_v * n_layer + to_l))
        return lax.ppermute(x, AXES, pairs)

    def over_layer(x, distance):
        return permute(x, lambda v, l: (v, l ^ distance))

    n_far = n_vocab // 2
    direct = n_far <= 4

    def over_vocab(x, far, flip):
        return permute(x, lambda v, l: (((v // 2 + far) % n_far) * 2 + ((v % 2) ^ flip), l))

    far_steps = sorted(range(1, n_far), key=lambda o: min(o, n_far - o))

    steps = [0] + far_steps

    def gather(block, given={}):
        if not direct:
            return {0: lax.all_gather(block, "vocab")}
        blocks = {("z", 0): block, **given}
        for o in far_steps:
            if ("z", o) not in blocks:
                blocks["z", o] = over_vocab(block, o, 0)
        for o in steps:
            if ("y", o) not in blocks:
                blocks["y", o] = over_vocab(blocks["z", o], 0, 1)
        return {key: blocks[key] for axis in "zy" for o in steps for key in [(axis, o)]}

    shared = [("z", far_steps[0]), ("y", 0)] if direct else []

    if direct:
        indices = [
            functools.partial(lambda o, flip, vocab, k: lax.rem(vocab // 2 + n_far - o, n_far) * 2 + lax.rem(vocab + flip, 2), o, flip)
            for flip in (0, 1)
            for o in steps
        ]
    else:
        indices = [lambda vocab, k: k]

    payload = pack(residual, gain)
    evens = sorted(range(0, n_layer, 2), reverse=True)
    remote = {}
    own = gather(payload)
    for e in evens[:-1]:
        given = {key: over_layer(own[key], e) for key in shared}
        remote[e] = gather(over_layer(payload, e), given)

    chunks = chunks_of(columns)
    codes, stats = {d: [] for d in range(n_layer)}, {d: [] for d in range(n_layer)}
    after = payload
    for e in evens:
        mine = own if e == 0 else remote[e]
        theirs = {key: over_layer(x, 1) for key, x in mine.items()}
        groups = [[x if x.ndim == 3 else x[None] for x in part.values()] for part in (mine, theirs)]
        joined = join(groups, indices, rows, after)
        for first, count in chunks if e else [(0, columns)]:
            new_codes, new_stats = logits_call(weights, joined, after, rows, first, count)
            after = new_stats[0]
            for d in (e, e + 1):
                code = new_codes[d - e]
                codes[d].append(over_layer(code, d) if d else code)
                stats[d].append(new_stats[d - e])
    for d in range(n_layer):
        stat = stats[d][0] if len(stats[d]) == 1 else jnp.concatenate(stats[d])
        stats[d] = over_layer(stat, d) if d else stat

    distances = [0, 1] + [d for e in evens[:-1] for d in (e, e + 1)]
    total = combine([stats[d] for d in distances])
    if direct:
        total = combine([total, over_vocab(total, 0, 1)])
        totals = [total] + [over_vocab(total, o, 0) for o in far_steps]
    else:
        totals = [lax.all_gather(total, "vocab", tiled=True)]

    if columns % 8:
        lse = row_lse([jnp.concatenate(totals)])
        pieces = []
        for d in range(n_layer):
            code, parts = jnp.concatenate(codes[d]), []
            for at in range(0, columns, TILE):
                factor, shift = decode_terms(stats[d], at // TILE, lse)
                parts.append(jnp.log(code[at : at + TILE].astype(F32)) * factor + shift)
            pieces.append(jnp.concatenate(parts))
        order = lax.axis_index("layer") ^ jnp.arange(n_layer)
        return jnp.take(jnp.stack(pieces), order, axis=0).reshape(n_layer * columns, rows).T

    early, late = [], []
    for d in distances:
        first = 0
        for array in codes[d]:
            for at in range(0, array.shape[0], CHUNK):
                early.append((array, (min(CHUNK, array.shape[0] - at), first + at, d, distances.index(d), at)))
            first += array.shape[0]
    early, late = early[:-1], early[-1:]
    out = None
    for part in (early, late):
        arrays, items = [], []
        for array, (count, first, d, source, at) in part:
            if not any(array is seen for seen in arrays):
                arrays.append(array)
            ref = [array is seen for seen in arrays].index(True)
            items.append((count, first, d, source, ref, at))
        out = write(arrays, items, [stats[d] for d in distances], totals, out, columns, n_layer * columns)
    return out.T


def solution(mesh):
    placed = (P("layer", "vocab"), P(None, "vocab"), P(None, ("vocab", "layer")))
    n_vocab, n_layer = mesh.shape["vocab"], mesh.shape["layer"]

    def body(residual, gain, unembed):
        return local(n_vocab, n_layer, residual, gain, unembed)

    mapped = jax.shard_map(body, mesh=mesh, in_specs=placed, out_specs=P("layer", "vocab"), check_vma=False)

    def step(residual, gain, unembed):
        return mapped(residual, gain, unembed)

    return step if n_vocab // 2 <= 4 else mapped
```

time: 570 us -> 351 us (0.62)
  blocking collectives: 291 us -> 0 us
  Pallas kernels: 0 us -> 117 us
  matrix products: 79.6 us -> 0 us
  starting transfers between devices: 0.04 us -> 71 us
  other arithmetic: 23.2 us -> 0.01 us
  between operations: 13.5 us -> 0.44 us
    all_to_all x1 -> x0, blocking collectives: 182 us -> none  [local(): lax.all_to_all(log_values, 'layer', split_axis=0, concat_axis=1, tiled=True)]
    ppermute x0 -> x45, waiting for transfers between devices: none -> 156 us  [permute(): return lax.ppermute(x, AXES, pairs)]
    all_gather x2 -> x0, waiting for transfers between devices: 153 us -> none  [the longest x1 77.7 us: local(): lax.all_gather(residual, 'vocab', axis=1, tiled=True)]
    pallas_call x0 -> x11, Pallas kernels: none -> 117 us  [the longest x4 96 us: logits_call(): pl.pallas_call(functools.partial(logits_kernel, n_groups, rows, columns,...]
    all_gather x3 -> x0, blocking collectives: 109 us -> none  [the longest x2 77.9 us: joined(): everything = jax.tree.map(lambda part: lax.all_gather(part, axis), shard)]
    dot_general x1 -> x0, matrix products: 79.6 us -> none  [local(): products = jnp.dot(scaled, unembed, preferred_element_type=jnp.float32)]
    ppermute x0 -> x45, starting transfers between devices: none -> 71 us  [permute(): return lax.ppermute(x, AXES, pairs)]
    reduce_sum x2 -> x0, other arithmetic: 15.6 us -> none  [the longest x1 8.41 us: local(): local_sums = jnp.sum(jnp.exp(logits - local_max[:, None]), axis=1)]
  transfers between devices with their start and end apart: 2 -> 45, of which waited for: 2 -> 14; matrix products, arithmetic and copies ran while one was open for 0% -> 0% of each run, Pallas kernels for 0% -> 16%
where the time goes in v1:
time: 351 us
  waiting for transfers between devices  156 us (44%)
  Pallas kernels  117 us (33%)
  starting transfers between devices  71 us (20%)
  local copies, waits for them, and re-layouts  6.51 us (2%)
    ppermute x45, waiting for transfers between devices, permute(): return lax.ppermute(x, AXES, pairs)  156 us
    pallas_call x4, Pallas kernels, logits_call(): pl.pallas_call(functools.partial(logits_kernel, n_groups, rows, columns,...  96 us
    ppermute x45, starting transfers between devices, permute(): return lax.ppermute(x, AXES, pairs)  71 us
    pallas_call x2, Pallas kernels, write(): pl.pallas_call(functools.partial(write_kernel, items, len(stats), len(tot...  12.9 us
  transfers between devices with their start and end apart: 45, of which 14 were waited for; matrix products, arithmetic and copies ran while one was open for 0% of the time, Pallas kernels for 16%

profile of v1, /device:TPU:0, one launch (start us, length us, event | category | flops | bytes accessed | tf_op | source)
XLA Modules:
  0.0 350.8 jit_solution(3518921481427895199)
XLA Ops:
  2.2 3.0 collective-permute-start.5
  8.3 2.6 collective-permute-start.20
  12.3 5.8 %collective-permute-done.5 = bf16[272,1024]{1,0:T(8,128)(2,1)S(1)} collective-permute-done((bf16[272,1024]{1,0:T(8,128)(2,1)}, bf16[272,1024]{1,0:T(8,128)(2,1)S(1)}, u32[]{:S(2)}, u32[]{:S(2)}) %collective-permute-start.5) | collective-permute-done | bytes 557088 | tf_op jit(solution)/shard_map/ppermute | solution.py:266
  19.8 3.1 collective-permute-done.1
  24.4 21.1 %collective-permute-done.20 = bf16[272,1024]{1,0:T(8,128)(2,1)S(1)} collective-permute-done((bf16[272,1024]{1,0:T(8,128)(2,1)}, bf16[272,1024]{1,0:T(8,128)(2,1)S(1)}, u32[]{:S(2)}, u32[]{:S(2)}) %collective-permute-start.20) | collective-permute-done | bytes 557088 | tf_op jit(solution)/shard_map/ppermute | solution.py:266
  45.4 3.5 %collective-permute-start.4 = (bf16[272,1024]{1,0:T(8,128)(2,1)S(1)}, bf16[272,1024]{1,0:T(8,128)(2,1)S(1)}, u32[]{:S(2)}, u32[]{:S(2)}) collective-permute-start(bf16[272,1024]{1,0:T(8,128)(2,1)S(1)} %collective-permute-done), channel_id=1, source_target_pairs={{0,16},{1,17},{2,18},{3,19},{4,20},{5,21},{6,22},{7,23},{8,24},{9,... | collective-permute-start | bytes 1671176 | tf_op jit(solution)/shard_map/ppermute | solution.py:266
  49.0 21.8 %collective-permute-start.3 = (bf16[272,1024]{1,0:T(8,128)(2,1)S(1)}, bf16[272,1024]{1,0:T(8,128)(2,1)S(1)}, u32[]{:S(2)}, u32[]{:S(2)}) collective-permute-start(bf16[272,1024]{1,0:T(8,128)(2,1)S(1)} %collective-permute-done), channel_id=1, source_target_pairs={{0,24},{1,25},{2,26},{3,27},{4,28},{5,29},{6,30},{7,31},{8,0},{9,1... | collective-permute-start | bytes 1671176 | tf_op jit(solution)/shard_map/ppermute | solution.py:266
  73.3 9.2 %collective-permute-done.3 = bf16[272,1024]{1,0:T(8,128)(2,1)S(1)} collective-permute-done((bf16[272,1024]{1,0:T(8,128)(2,1)S(1)}, bf16[272,1024]{1,0:T(8,128)(2,1)S(1)}, u32[]{:S(2)}, u32[]{:S(2)}) %collective-permute-start.3) | collective-permute-done | bytes 557088 | tf_op jit(solution)/shard_map/ppermute | solution.py:266
  83.6 3.2 collective-permute-done.7
  86.8 11.9 %collective-permute-done.9 = bf16[272,1024]{1,0:T(8,128)(2,1)S(1)} collective-permute-done((bf16[272,1024]{1,0:T(8,128)(2,1)S(1)}, bf16[272,1024]{1,0:T(8,128)(2,1)S(1)}, u32[]{:S(2)}, u32[]{:S(2)}) %collective-permute-start.9) | collective-permute-done | bytes 557088 | tf_op jit(solution)/shard_map/ppermute | solution.py:266
  98.8 11.0 %collective-permute-done.8 = bf16[272,1024]{1,0:T(8,128)(2,1)S(1)} collective-permute-done((bf16[272,1024]{1,0:T(8,128)(2,1)S(1)}, bf16[272,1024]{1,0:T(8,128)(2,1)S(1)}, u32[]{:S(2)}, u32[]{:S(2)}) %collective-permute-start.8) | collective-permute-done | bytes 557088 | tf_op jit(solution)/shard_map/ppermute | solution.py:266
  115.1 13.9 %shard_map.39 = (bf16[1024,256]{1,0:T(8,128)(2,1)}, bf16[1024,256]{1,0:T(8,128)(2,1)S(1)}, f32[16,256]{1,0:T(8,128)S(1)}, f32[16,256]{1,0:T(8,128)S(1)}) custom-call(bf16[4008,8192]{1,0:T(8,128)(2,1)} %bitcast.66, bf16[512,8192]{1,0:T(8,128)(2,1)S(1)} %get-tuple-element.25.a_ref, f32[8,512]{1,0:T(8,128)S(1)} %get-tuple-element.26.inverse_ref, ...), custom_call_target="tpu_custom_call" | custom-call | flops 8589934592 | bytes 25165824 | tf_op jit(solution)/shard_map/pallas_call | solution.py:146
  130.2 18.3 %shard_map.40 = (bf16[1536,256]{1,0:T(8,128)(2,1)S(1)}, bf16[1536,256]{1,0:T(8,128)(2,1)S(1)}, f32[24,256]{1,0:T(8,128)S(1)}, f32[24,256]{1,0:T(8,128)S(1)}) custom-call(bf16[4008,8192]{1,0:T(8,128)(2,1)} %bitcast.67, bf16[512,8192]{1,0:T(8,128)(2,1)S(1)} %get-tuple-element.25.a_ref, f32[8,512]{1,0:T(8,128)S(1)} %get-tuple-element.26.inverse_ref, ...), custom_call_target="tpu_custom_call" | custom-call | flops 12884901888 | bytes 33554432 | tf_op jit(solution)/shard_map/pallas_call | solution.py:146
  150.4 19.2 %shard_map.41 = (bf16[1448,256]{1,0:T(8,128)(2,1)S(1)}, bf16[1448,256]{1,0:T(8,128)(2,1)S(1)}, f32[24,256]{1,0:T(8,128)S(1)}, f32[24,256]{1,0:T(8,128)S(1)}) custom-call(bf16[4008,8192]{1,0:T(8,128)(2,1)} %bitcast.68, bf16[512,8192]{1,0:T(8,128)(2,1)S(1)} %get-tuple-element.25.a_ref, f32[8,512]{1,0:T(8,128)S(1)} %get-tuple-element.26.inverse_ref, ...), custom_call_target="tpu_custom_call" | custom-call | flops 12146704384 | bytes 32112640 | tf_op jit(solution)/shard_map/pallas_call | solution.py:146
  171.2 44.6 %shard_map.43 = (bf16[4008,256]{1,0:T(8,128)(2,1)S(1)}, bf16[4008,256]{1,0:T(8,128)(2,1)S(1)}, f32[64,256]{1,0:T(8,128)S(1)}, f32[64,256]{1,0:T(8,128)S(1)}) custom-call(bf16[4008,8192]{1,0:T(8,128)(2,1)} %bitcast.69, bf16[512,8192]{1,0:T(8,128)(2,1)S(1)} %get-tuple-element.31.a_ref, f32[8,512]{1,0:T(8,128)S(1)} %get-tuple-element.32.inverse_ref, ...), custom_call_target="tpu_custom_call" | custom-call | flops 33621540864 | bytes 74055680 | tf_op jit(solution)/shard_map/pallas_call | solution.py:146
  221.7 24.0 %collective-permute-done.33.refs_2_.refs_10_.refs_3_ = f32[64,256]{1,0:T(8,128)S(1)} collective-permute-done((f32[64,256]{1,0:T(8,128)S(1)}, f32[64,256]{1,0:T(8,128)S(1)}, u32[]{:S(2)}, u32[]{:S(2)}) %collective-permute-start.33) | collective-permute-done | bytes 65568 | tf_op jit(solution)/shard_map/ppermute | solution.py:266
  250.0 3.0 collective-permute-done.35.refs_1_
  257.0 10.6 %collective-permute-start.37 = (f32[8,256]{1,0:T(8,128)}, f32[8,256]{1,0:T(8,128)S(1)}, u32[]{:S(2)}, u32[]{:S(2)}) collective-permute-start(f32[8,256]{1,0:T(8,128)} %shard_map.45.refs_12_.refs_5_), channel_id=1, source_target_pairs={{0,24},{1,25},{2,26},{3,27},{4,28},{5,29},{6,30},{7,31},{8,0},{9,1... | collective-permute-start | bytes 24584 | tf_op jit(solution)/shard_map/ppermute | solution.py:266
  267.6 2.4 collective-permute-start.36
  271.6 2.7 collective-permute-done.36.refs_13_.refs_6_
  277.5 45.1 %collective-permute-done.18.refs_7_.refs_0_ = bf16[1448,256]{1,0:T(8,128)(2,1)S(1)} collective-permute-done((bf16[1448,256]{1,0:T(8,128)(2,1)}, bf16[1448,256]{1,0:T(8,128)(2,1)S(1)}, u32[]{:S(2)}, u32[]{:S(2)}) %collective-permute-start.18) | collective-permute-done | bytes 741408 | tf_op jit(solution)/shard_map/ppermute | solution.py:266
  322.6 13.7 %collective-permute-done.42.refs_4_ = bf16[1448,256]{1,0:T(8,128)(2,1)S(1)} collective-permute-done((bf16[1448,256]{1,0:T(8,128)(2,1)}, bf16[1448,256]{1,0:T(8,128)(2,1)S(1)}, u32[]{:S(2)}, u32[]{:S(2)}) %collective-permute-start.42) | collective-permute-done | bytes 741408 | tf_op jit(solution)/shard_map/ppermute | solution.py:266
  337.7 10.1 %shard_map.46.refs_9_ = f32[16032,256]{1,0:T(8,128)} custom-call(bf16[4008,256]{1,0:T(8,128)(2,1)} %copy-done.2, bf16[4008,256]{1,0:T(8,128)(2,1)} %collective-permute-done.39.refs_1_, bf16[1024,256]{1,0:T(8,128)(2,1)} %collective-permute-done.40.refs_2_, bf16[1536,256]{1,0:T(8,128)(2,1)} %copy-done.8, bf16[1448,256]{1,0:T(8,128)(2,1)} %copy-done.10, ...), custom_call_target="tpu_custom_call" | custom-call | bytes 23973888 | tf_op jit(solution)/shard_map/pallas_call | solution.py:234
  347.8 2.8 shard_map.47
  (115 shorter events, 43.7 us)
Async XLA Ops:
  8.3 37.1 %collective-permute-start.20 = (bf16[272,1024]{1,0:T(8,128)(2,1)}, bf16[272,1024]{1,0:T(8,128)(2,1)S(1)}, u32[]{:S(2)}, u32[]{:S(2)}) collective-permute-start(bf16[272,1024]{1,0:T(8,128)(2,1)} %shard_map.37.refs_16_.after_ref), channel_id=1, source_target_pairs={{0,16},{1,17},{2,18},{3,19},{4,20},{5,21},{6,22},{7,23},{8,24},{9,... | collective-permute-start | bytes 1671176 | tf_op jit(solution)/shard_map/ppermute | solution.py:266
  10.9 38.1 %collective-permute-start.19 = (bf16[272,1024]{1,0:T(8,128)(2,1)}, bf16[272,1024]{1,0:T(8,128)(2,1)S(1)}, u32[]{:S(2)}, u32[]{:S(2)}) collective-permute-start(bf16[272,1024]{1,0:T(8,128)(2,1)} %shard_map.37.refs_16_.after_ref), channel_id=1, source_target_pairs={{0,24},{1,25},{2,26},{3,27},{4,28},{5,29},{6,30},{7,31},{8,0},{9,1... | collective-permute-start | bytes 1671176 | tf_op jit(solution)/shard_map/ppermute | solution.py:266
  18.1 52.7 %collective-permute-start.6 = (bf16[272,1024]{1,0:T(8,128)(2,1)S(1)}, bf16[272,1024]{1,0:T(8,128)(2,1)S(1)}, u32[]{:S(2)}, u32[]{:S(2)}) collective-permute-start(bf16[272,1024]{1,0:T(8,128)(2,1)S(1)} %collective-permute-done.5), channel_id=1, source_target_pairs={{0,2},{1,3},{2,0},{3,1},{4,6},{5,7},{6,4},{7,5},{8,10},{9,11},{10,... | collective-permute-start | bytes 1671176 | tf_op jit(solution)/shard_map/ppermute | solution.py:266
  22.9 47.9 %collective-permute-start.2 = (bf16[272,1024]{1,0:T(8,128)(2,1)S(1)}, bf16[272,1024]{1,0:T(8,128)(2,1)S(1)}, u32[]{:S(2)}, u32[]{:S(2)}) collective-permute-start(bf16[272,1024]{1,0:T(8,128)(2,1)S(1)} %collective-permute-done.1), channel_id=1, source_target_pairs={{0,2},{1,3},{2,0},{3,1},{4,6},{5,7},{6,4},{7,5},{8,10},{9,11},{10,... | collective-permute-start | bytes 1671176 | tf_op jit(solution)/shard_map/ppermute | solution.py:266
  24.4 46.9 %collective-permute-start.10 = (bf16[272,1024]{1,0:T(8,128)(2,1)S(1)}, bf16[272,1024]{1,0:T(8,128)(2,1)S(1)}, u32[]{:S(2)}, u32[]{:S(2)}) collective-permute-start(bf16[272,1024]{1,0:T(8,128)(2,1)S(1)} %collective-permute-done), channel_id=1, source_target_pairs={{0,1},{1,0},{2,3},{3,2},{4,5},{5,4},{6,7},{7,6},{8,9},{9,8},{10,11... | collective-permute-start | bytes 1671176 | tf_op jit(solution)/shard_map/ppermute | solution.py:266
  45.4 26.4 %collective-permute-start.4 = (bf16[272,1024]{1,0:T(8,128)(2,1)S(1)}, bf16[272,1024]{1,0:T(8,128)(2,1)S(1)}, u32[]{:S(2)}, u32[]{:S(2)}) collective-permute-start(bf16[272,1024]{1,0:T(8,128)(2,1)S(1)} %collective-permute-done), channel_id=1, source_target_pairs={{0,16},{1,17},{2,18},{3,19},{4,20},{5,21},{6,22},{7,23},{8,24},{9,... | collective-permute-start | bytes 1671176 | tf_op jit(solution)/shard_map/ppermute | solution.py:266
  49.0 33.6 %collective-permute-start.3 = (bf16[272,1024]{1,0:T(8,128)(2,1)S(1)}, bf16[272,1024]{1,0:T(8,128)(2,1)S(1)}, u32[]{:S(2)}, u32[]{:S(2)}) collective-permute-start(bf16[272,1024]{1,0:T(8,128)(2,1)S(1)} %collective-permute-done), channel_id=1, source_target_pairs={{0,24},{1,25},{2,26},{3,27},{4,28},{5,29},{6,30},{7,31},{8,0},{9,1... | collective-permute-start | bytes 1671176 | tf_op jit(solution)/shard_map/ppermute | solution.py:266
  71.8 26.9 %collective-permute-start.9 = (bf16[272,1024]{1,0:T(8,128)(2,1)S(1)}, bf16[272,1024]{1,0:T(8,128)(2,1)S(1)}, u32[]{:S(2)}, u32[]{:S(2)}) collective-permute-start(bf16[272,1024]{1,0:T(8,128)(2,1)S(1)} %collective-permute-done.4), channel_id=1, source_target_pairs={{0,4},{1,5},{2,6},{3,7},{4,0},{5,1},{6,2},{7,3},{8,12},{9,13},{10,... | collective-permute-start | bytes 1671176 | tf_op jit(solution)/shard_map/ppermute | solution.py:266
  82.6 27.2 %collective-permute-start.8 = (bf16[272,1024]{1,0:T(8,128)(2,1)S(1)}, bf16[272,1024]{1,0:T(8,128)(2,1)S(1)}, u32[]{:S(2)}, u32[]{:S(2)}) collective-permute-start(bf16[272,1024]{1,0:T(8,128)(2,1)S(1)} %collective-permute-done.3), channel_id=1, source_target_pairs={{0,4},{1,5},{2,6},{3,7},{4,0},{5,1},{6,2},{7,3},{8,12},{9,13},{10,... | collective-permute-start | bytes 1671176 | tf_op jit(solution)/shard_map/ppermute | solution.py:266
  83.1 26.7 %collective-permute-start.13 = (bf16[272,1024]{1,0:T(8,128)(2,1)S(1)}, bf16[272,1024]{1,0:T(8,128)(2,1)S(1)}, u32[]{:S(2)}, u32[]{:S(2)}) collective-permute-start(bf16[272,1024]{1,0:T(8,128)(2,1)S(1)} %collective-permute-done.4), channel_id=1, source_target_pairs={{0,1},{1,0},{2,3},{3,2},{4,5},{5,4},{6,7},{7,6},{8,9},{9,8},{10,11... | collective-permute-start | bytes 1671176 | tf_op jit(solution)/shard_map/ppermute | solution.py:266
  83.1 27.2 %collective-permute-start.12 = (bf16[272,1024]{1,0:T(8,128)(2,1)S(1)}, bf16[272,1024]{1,0:T(8,128)(2,1)S(1)}, u32[]{:S(2)}, u32[]{:S(2)}) collective-permute-start(bf16[272,1024]{1,0:T(8,128)(2,1)S(1)} %collective-permute-done.3), channel_id=1, source_target_pairs={{0,1},{1,0},{2,3},{3,2},{4,5},{5,4},{6,7},{7,6},{8,9},{9,8},{10,11... | collective-permute-start | bytes 1671176 | tf_op jit(solution)/shard_map/ppermute | solution.py:266
  110.3 39.0 %collective-permute-start.27 = (bf16[272,1024]{1,0:T(8,128)(2,1)S(1)}, bf16[272,1024]{1,0:T(8,128)(2,1)S(1)}, u32[]{:S(2)}, u32[]{:S(2)}) collective-permute-start(bf16[272,1024]{1,0:T(8,128)(2,1)S(1)} %collective-permute-done.20), channel_id=1, source_target_pairs={{0,1},{1,0},{2,3},{3,2},{4,5},{5,4},{6,7},{7,6},{8,9},{9,8},{10,11... | collective-permute-start | bytes 1671176 | tf_op jit(solution)/shard_map/ppermute | solution.py:266
  110.4 39.0 %collective-permute-start.23 = (bf16[272,1024]{1,0:T(8,128)(2,1)S(1)}, bf16[272,1024]{1,0:T(8,128)(2,1)S(1)}, u32[]{:S(2)}, u32[]{:S(2)}) collective-permute-start(bf16[272,1024]{1,0:T(8,128)(2,1)S(1)} %collective-permute-done.20), channel_id=1, source_target_pairs={{0,4},{1,5},{2,6},{3,7},{4,0},{5,1},{6,2},{7,3},{8,12},{9,13},{10,... | collective-permute-start | bytes 1671176 | tf_op jit(solution)/shard_map/ppermute | solution.py:266
  110.9 39.0 %collective-permute-start.26 = (bf16[272,1024]{1,0:T(8,128)(2,1)S(1)}, bf16[272,1024]{1,0:T(8,128)(2,1)S(1)}, u32[]{:S(2)}, u32[]{:S(2)}) collective-permute-start(bf16[272,1024]{1,0:T(8,128)(2,1)S(1)} %collective-permute-done.19), channel_id=1, source_target_pairs={{0,1},{1,0},{2,3},{3,2},{4,5},{5,4},{6,7},{7,6},{8,9},{9,8},{10,11... | collective-permute-start | bytes 1671176 | tf_op jit(solution)/shard_map/ppermute | solution.py:266
  111.7 38.2 %collective-permute-start.22 = (bf16[272,1024]{1,0:T(8,128)(2,1)S(1)}, bf16[272,1024]{1,0:T(8,128)(2,1)S(1)}, u32[]{:S(2)}, u32[]{:S(2)}) collective-permute-start(bf16[272,1024]{1,0:T(8,128)(2,1)S(1)} %collective-permute-done.19), channel_id=1, source_target_pairs={{0,4},{1,5},{2,6},{3,7},{4,0},{5,1},{6,2},{7,3},{8,12},{9,13},{10,... | collective-permute-start | bytes 1671176 | tf_op jit(solution)/shard_map/ppermute | solution.py:266
  217.8 118.4 %collective-permute-start.39 = (bf16[4008,256]{1,0:T(8,128)(2,1)S(1)}, bf16[4008,256]{1,0:T(8,128)(2,1)}, u32[]{:S(2)}, u32[]{:S(2)}) collective-permute-start(bf16[4008,256]{1,0:T(8,128)(2,1)S(1)} %get-tuple-element.39), channel_id=1, source_target_pairs={{0,1},{1,0},{2,3},{3,2},{4,5},{5,4},{6,7},{7,6},{8,9},{9,8},{10,11... | collective-permute-start | bytes 6156296 | tf_op jit(solution)/shard_map/ppermute | solution.py:266
  218.2 56.0 %collective-permute-start.40 = (bf16[1024,256]{1,0:T(8,128)(2,1)}, bf16[1024,256]{1,0:T(8,128)(2,1)}, u32[]{:S(2)}, u32[]{:S(2)}) collective-permute-start(bf16[1024,256]{1,0:T(8,128)(2,1)} %get-tuple-element.40), channel_id=1, source_target_pairs={{0,2},{1,3},{2,0},{3,1},{4,6},{5,7},{6,4},{7,5},{8,10},{9,11},{10,... | collective-permute-start | bytes 1572872 | tf_op jit(solution)/shard_map/ppermute | solution.py:266
  219.7 56.3 %collective-permute-start.43 = (bf16[1024,256]{1,0:T(8,128)(2,1)S(1)}, bf16[1024,256]{1,0:T(8,128)(2,1)}, u32[]{:S(2)}, u32[]{:S(2)}) collective-permute-start(bf16[1024,256]{1,0:T(8,128)(2,1)S(1)} %get-tuple-element.43), channel_id=1, source_target_pairs={{0,3},{1,2},{2,1},{3,0},{4,7},{5,6},{6,5},{7,4},{8,11},{9,10},{10,... | collective-permute-start | bytes 1572872 | tf_op jit(solution)/shard_map/ppermute | solution.py:266
  219.7 26.0 %collective-permute-start.33 = (f32[64,256]{1,0:T(8,128)S(1)}, f32[64,256]{1,0:T(8,128)S(1)}, u32[]{:S(2)}, u32[]{:S(2)}) collective-permute-start(f32[64,256]{1,0:T(8,128)S(1)} %pad_maximum_fusion), channel_id=1, source_target_pairs={{0,2},{1,3},{2,0},{3,1},{4,6},{5,7},{6,4},{7,5},{8,10},{9,11},{10,... | collective-permute-start | bytes 196616 | tf_op jit(solution)/shard_map/ppermute | solution.py:266
  221.2 24.5 %collective-permute-start.34 = (f32[64,256]{1,0:T(8,128)S(1)}, f32[64,256]{1,0:T(8,128)S(1)}, u32[]{:S(2)}, u32[]{:S(2)}) collective-permute-start(f32[64,256]{1,0:T(8,128)S(1)} %pad_maximum_fusion.1), channel_id=1, source_target_pairs={{0,3},{1,2},{2,1},{3,0},{4,7},{5,6},{6,5},{7,4},{8,11},{9,10},{10,... | collective-permute-start | bytes 196616 | tf_op jit(solution)/shard_map/ppermute | solution.py:266
  270.1 66.1 %collective-permute-start.41 = (bf16[1536,256]{1,0:T(8,128)(2,1)}, bf16[1536,256]{1,0:T(8,128)(2,1)S(1)}, u32[]{:S(2)}, u32[]{:S(2)}) collective-permute-start(bf16[1536,256]{1,0:T(8,128)(2,1)} %copy-done.4), channel_id=1, source_target_pairs={{0,2},{1,3},{2,0},{3,1},{4,6},{5,7},{6,4},{7,5},{8,10},{9,11},{10,... | collective-permute-start | bytes 2359304 | tf_op jit(solution)/shard_map/ppermute | solution.py:266
  274.2 62.0 %collective-permute-start.44 = (bf16[1536,256]{1,0:T(8,128)(2,1)S(1)}, bf16[1536,256]{1,0:T(8,128)(2,1)S(1)}, u32[]{:S(2)}, u32[]{:S(2)}) collective-permute-start(bf16[1536,256]{1,0:T(8,128)(2,1)S(1)} %get-tuple-element.44), channel_id=1, source_target_pairs={{0,3},{1,2},{2,1},{3,0},{4,7},{5,6},{6,5},{7,4},{8,11},{9,10},{10,... | collective-permute-start | bytes 2359304 | tf_op jit(solution)/shard_map/ppermute | solution.py:266
  274.2 48.3 %collective-permute-start.18 = (bf16[1448,256]{1,0:T(8,128)(2,1)}, bf16[1448,256]{1,0:T(8,128)(2,1)S(1)}, u32[]{:S(2)}, u32[]{:S(2)}) collective-permute-start(bf16[1448,256]{1,0:T(8,128)(2,1)} %copy-done.6), channel_id=1, source_target_pairs={{0,3},{1,2},{2,1},{3,0},{4,7},{5,6},{6,5},{7,4},{8,11},{9,10},{10,... | collective-permute-start | bytes 2224136 | tf_op jit(solution)/shard_map/ppermute | solution.py:266
  276.0 60.2 %collective-permute-start.42 = (bf16[1448,256]{1,0:T(8,128)(2,1)}, bf16[1448,256]{1,0:T(8,128)(2,1)S(1)}, u32[]{:S(2)}, u32[]{:S(2)}) collective-permute-start(bf16[1448,256]{1,0:T(8,128)(2,1)} %copy-done.5), channel_id=1, source_target_pairs={{0,2},{1,3},{2,0},{3,1},{4,6},{5,7},{6,4},{7,5},{8,10},{9,11},{10,... | collective-permute-start | bytes 2224136 | tf_op jit(solution)/shard_map/ppermute | solution.py:266
  (39 other events, 626.5 us)

commit v2 on v1

--- a/solution.py
+++ b/solution.py
@@ -11,14 +11,15 @@
 EPS = 1e-05
 TILE = 512
 CHUNK = 1024
-FIRST, LATER = 1024, 1536
+EDGES = (1536,)
+AHEAD = 0
 DEPTH = 4
 SPAN = 250.0
 LN2 = 0.6931471805599453
 AXES = ("vocab", "layer")
 F32 = jnp.float32
 BF16 = jnp.bfloat16
-VMEM_LIMIT = 28 * 1024 * 1024
+VMEM_LIMIT, SPLIT_LIMIT, PART_LIMIT = 28 * 1024 * 1024, 20 * 1024 * 1024, 14 * 1024 * 1024
 JOIN_LIMIT = 12 * 1024 * 1024
 NT = (((1,), (1,)), ((), ()))
 HBM = pl.BlockSpec(memory_space=pl.ANY)
@@ -66,10 +67,11 @@
     )(residual, gain)
 
 
-def join_kernel(n_groups, stacks, indices, rows, *refs):
+def join_kernel(n_groups, all_features, stacks, indices, rows, *refs):
     n = len(stacks)
     block_refs = refs[: n * n_groups]
-    a_ref, inverse_ref, sums_ref, sem = refs[n * n_groups + 1 :]
+    before_ref = refs[n * n_groups + 1]
+    a_ref, total_ref, inverse_ref, sums_ref, sem = refs[n * n_groups + 2 :]
     width = block_refs[0].shape[2]
     piece, slots, extra = sum_slots(rows, width)
     vocab = lax.axis_index("vocab")
@@ -79,7 +81,7 @@
         for j in range(n):
             ref = block_refs[g * n + j]
             for k in range(stacks[j]):
-                at = pl.multiple_of(indices[j](vocab, k) * width, width)
+                at = slot * width if indices is None else pl.multiple_of(indices[j](vocab, k) * width, width)
                 copies.append(pltpu.make_async_copy(ref.at[k, pl.ds(0, rows), :], a_ref.at[pl.ds(g * rows, rows), pl.ds(at, width)], sem))
                 copies.append(pltpu.make_async_copy(ref.at[k, pl.ds(rows, extra), :], sums_ref.at[g, slot], sem))
                 slot += 1
@@ -93,32 +95,79 @@
             for part, at, row, lane in slots:
                 if at == row_first:
                     total = total + jnp.sum(sums_ref[g, :, pl.ds(row, 16), pl.ds(lane, piece)].astype(F32), axis=0)
-            features = width * sum(stacks)
-            inverse = lax.rsqrt(total / features + EPS)
-            inverse_ref[:, pl.ds(g * rows + row_first, piece)] = inverse[0:8, :]
-
-
-def join(groups, indices, rows, after):
+            lanes = pl.ds(g * rows + row_first, piece)
+            total = total[0:8, :] + before_ref[:, lanes]
+            total_ref[:, lanes] = total
+            inverse_ref[:, lanes] = lax.rsqrt(total / all_features + EPS)
+
+
+def join(groups, all_features, indices, rows, after, before):
     stacks = [block.shape[0] for block in groups[0]]
     width = groups[0][0].shape[2]
     extra, features = sum_slots(rows, width)[2], width * sum(stacks)
     total = rows * len(groups)
+    if before is None:
+        before = jnp.zeros((8, total), F32)
     return pl.pallas_call(
-        functools.partial(join_kernel, len(groups), stacks, indices, rows),
-        out_shape=[jax.ShapeDtypeStruct((total, features), BF16), jax.ShapeDtypeStruct((8, total), F32)],
-        in_specs=[HBM] * (len(stacks) * len(groups) + 1),
-        out_specs=[VMEM, VMEM],
+        functools.partial(join_kernel, len(groups), all_features, stacks, indices, rows),
+        out_shape=[jax.ShapeDtypeStruct((total, features), BF16)] + [jax.ShapeDtypeStruct((8, total), F32)] * 2,
+        in_specs=[HBM] * (len(stacks) * len(groups) + 1) + [VMEM],
+        out_specs=[VMEM] * 3,
         scratch_shapes=[pltpu.VMEM((len(groups), sum(stacks), extra, width), BF16), pltpu.SemaphoreType.DMA],
         compiler_params=pltpu.CompilerParams(vmem_limit_bytes=JOIN_LIMIT),
         cost_estimate=pl.CostEstimate(flops=total * features, bytes_accessed=4 * total * features, transcendentals=0),
-    )(*[block for group in groups for block in group], after)
-
-
-def logits_kernel(n_groups, rows, columns, first, partial, w_ref, a_ref, inverse_ref, after_ref, *outs):
-    del after_ref
+    )(*[block for group in groups for block in group], after, before)
+
+
+def multiply(w_refs, a_ref):
+    width = w_refs[0].shape[1]
+    terms = [
+        lax.dot_general(w_ref[...], a_ref[:, i * width : (i + 1) * width], NT, preferred_element_type=F32)
+        for i, w_ref in enumerate(w_refs)
+    ]
+    return functools.reduce(jnp.add, terms)
+
+
+def part_kernel(n_blocks, place_ref, *refs):
+    del place_ref
+    refs[-1][...] = multiply(refs[:n_blocks], refs[n_blocks])
+
+
+def weight_specs(base, places, features):
+    if places is None:
+        return [pl.BlockSpec((TILE, features), lambda i, place: (base + i, 0))]
+    width = features // places.shape[0]
+    return [pl.BlockSpec((TILE, width), lambda i, place, j=j: (base + i, place[j])) for j in range(places.shape[0])]
+
+
+def part_call(weights, scaled, places, after, first, count):
+    rows, features = scaled.shape
+    specs = weight_specs(first // TILE, places, features)
+    return pl.pallas_call(
+        functools.partial(part_kernel, len(specs)),
+        grid_spec=pltpu.PrefetchScalarGridSpec(
+            num_scalar_prefetch=1,
+            grid=(pl.cdiv(count, TILE),),
+            in_specs=specs + [VMEM, HBM],
+            out_specs=pl.BlockSpec((TILE, rows), lambda i, place: (i, 0)),
+        ),
+        out_shape=jax.ShapeDtypeStruct((count, rows), F32),
+        compiler_params=pltpu.CompilerParams(vmem_limit_bytes=PART_LIMIT),
+        cost_estimate=pl.CostEstimate(
+            flops=2 * count * features * rows, bytes_accessed=2 * count * features + 4 * rows * count, transcendentals=0
+        ),
+    )(places, *[weights] * len(specs), scaled, after)
+
+
+def logits_kernel(n_blocks, n_groups, rows, columns, first, partial, has_part, place_ref, *refs):
+    del place_ref
+    a_ref, inverse_ref = refs[n_blocks : n_blocks + 2]
+    outs = refs[n_blocks + 3 + has_part :]
     code_refs, stat_refs = outs[:n_groups], outs[n_groups:]
     step = pl.program_id(0)
-    products = lax.dot_general(w_ref[...], a_ref[...], NT, preferred_element_type=F32)
+    products = multiply(refs[:n_blocks], a_ref)
+    if has_part:
+        products = products + refs[n_blocks + 3][...]
     logits = products * inverse_ref[0:1, :]
     if partial:
         entry = first + step * TILE + lax.broadcasted_iota(jnp.int32, logits.shape, 0)
@@ -138,24 +187,32 @@
         stat_refs[g][...] = stats[:, g * rows : (g + 1) * rows]
 
 
-def logits_call(weights, joined, after, rows, first, count):
-    scaled, inverse = joined
-    columns, features = weights.shape
+def logits_call(weights, joined, places, part, after, rows, first, count):
+    scaled, _, inverse = joined
+    columns, features = weights.shape[0], scaled.shape[1]
     n_groups, tiles = scaled.shape[0] // rows, pl.cdiv(count, TILE)
-    base = first // TILE
+    specs = weight_specs(first // TILE, places, features)
+    if places is None:
+        places = jnp.zeros((1,), jnp.int32)
+    n_blocks, has_part = len(specs), int(part is not None)
+    specs = specs + [VMEM, VMEM, HBM] + [pl.BlockSpec((TILE, scaled.shape[0]), lambda i, place: (i, 0))] * has_part
     out = pl.pallas_call(
-        functools.partial(logits_kernel, n_groups, rows, columns, first, count % TILE != 0),
-        grid=(tiles,),
-        in_specs=[pl.BlockSpec((TILE, features), lambda i: (base + i, 0)), VMEM, VMEM, HBM],
-        out_specs=[pl.BlockSpec((TILE, rows), lambda i: (i, 0))] * n_groups + [pl.BlockSpec((8, rows), lambda i: (i, 0))] * n_groups,
+        functools.partial(logits_kernel, n_blocks, n_groups, rows, columns, first, count % TILE != 0, has_part),
+        grid_spec=pltpu.PrefetchScalarGridSpec(
+            num_scalar_prefetch=1,
+            grid=(tiles,),
+            in_specs=specs,
+            out_specs=[pl.BlockSpec((TILE, rows), lambda i, place: (i, 0))] * n_groups
+            + [pl.BlockSpec((8, rows), lambda i, place: (i, 0))] * n_groups,
+        ),
         out_shape=[jax.ShapeDtypeStruct((count, rows), BF16)] * n_groups + [jax.ShapeDtypeStruct((8 * tiles, rows), F32)] * n_groups,
-        compiler_params=pltpu.CompilerParams(vmem_limit_bytes=VMEM_LIMIT),
+        compiler_params=pltpu.CompilerParams(vmem_limit_bytes=SPLIT_LIMIT if has_part else VMEM_LIMIT),
         cost_estimate=pl.CostEstimate(
             flops=2 * count * features * rows * n_groups,
             bytes_accessed=2 * count * features + 2 * rows * n_groups * features,
             transcendentals=2 * count * rows * n_groups,
         ),
-    )(weights, scaled, inverse, after)
+    )(places, *[weights] * n_blocks, scaled, inverse, after, *([part] if has_part else []))
     return out[:n_groups], out[n_groups:]
 
 
@@ -248,14 +305,14 @@
 
 
 def chunks_of(columns):
-    edges = [0] + list(range(FIRST, columns, LATER)) + [columns]
+    edges = [0] + [edge for edge in EDGES if edge < columns] + [columns]
     return [(first, last - first) for first, last in zip(edges, edges[1:])]
 
 
 def local(n_vocab, n_layer, residual, gain, unembed):
     rows = residual.shape[0]
     weights = unembed.T
-    columns = weights.shape[0]
+    columns, features = weights.shape
 
     def permute(x, move):
         pairs = []
@@ -288,18 +345,20 @@
         for o in steps:
             if ("y", o) not in blocks:
                 blocks["y", o] = over_vocab(blocks["z", o], 0, 1)
-        return {key: blocks[key] for axis in "zy" for o in steps for key in [(axis, o)]}
+        return blocks
 
     shared = [("z", far_steps[0]), ("y", 0)] if direct else []
 
-    if direct:
-        indices = [
-            functools.partial(lambda o, flip, vocab, k: lax.rem(vocab // 2 + n_far - o, n_far) * 2 + lax.rem(vocab + flip, 2), o, flip)
-            for flip in (0, 1)
-            for o in steps
-        ]
-    else:
-        indices = [lambda vocab, k: k]
+    def index_of(key):
+        flip, o = "zy".index(key[0]), key[1]
+        return lambda vocab, k: lax.rem(vocab // 2 + n_far - o, n_far) * 2 + lax.rem(vocab + flip, 2)
+
+    every = [(axis, o) for axis in "zy" for o in steps] if direct else [0]
+    indices = [index_of(key) for key in every] if direct else [lambda vocab, k: k]
+    early = []
+
+    def places_of(keys):
+        return jnp.stack([index_of(key)(lax.axis_index("vocab"), 0) for key in keys]).astype(jnp.int32)
 
     payload = pack(residual, gain)
     evens = sorted(range(0, n_layer, 2), reverse=True)
@@ -315,10 +374,28 @@
     for e in evens:
         mine = own if e == 0 else remote[e]
         theirs = {key: over_layer(x, 1) for key, x in mine.items()}
-        groups = [[x if x.ndim == 3 else x[None] for x in part.values()] for part in (mine, theirs)]
-        joined = join(groups, indices, rows, after)
-        for first, count in chunks if e else [(0, columns)]:
-            new_codes, new_stats = logits_call(weights, joined, after, rows, first, count)
+
+        def blocks_of(keys):
+            return [[part[key] if part[key].ndim == 3 else part[key][None] for key in keys] for part in (mine, theirs)]
+
+        parts, places = [None] * len(chunks), None
+        if e and early:
+            late = [key for key in every if key not in early]
+            first_half, sums, _ = join(blocks_of(early), features, None, rows, after, None)
+            for i, (first, count) in enumerate(chunks[:AHEAD]):
+                parts[i] = part_call(weights, first_half, places_of(early), after, first, count)
+                after = parts[i]
+            joined = join(blocks_of(late), features, None, rows, after, sums)
+            places = places_of(late)
+        else:
+            joined = join(blocks_of(every), features, indices, rows, after, None)
+        for i, (first, count) in enumerate(chunks if e else [(0, columns)]):
+            if places is not None and parts[i] is None:
+                parts[i] = part_call(weights, first_half, places_of(early), after, first, count)
+                after = parts[i]
+            new_codes, new_stats = logits_call(
+                weights, joined, places, parts[i] if e else None, after, rows, first, count
+            )
             after = new_stats[0]
             for d in (e, e + 1):
                 code = new_codes[d - e]
@@ -348,16 +425,15 @@
         order = lax.axis_index("layer") ^ jnp.arange(n_layer)
         return jnp.take(jnp.stack(pieces), order, axis=0).reshape(n_layer * columns, rows).T
 
-    early, late = [], []
+    items_all = []
     for d in distances:
         first = 0
         for array in codes[d]:
             for at in range(0, array.shape[0], CHUNK):
-                early.append((array, (min(CHUNK, array.shape[0] - at), first + at, d, distances.index(d), at)))
+                items_all.append((array, (min(CHUNK, array.shape[0] - at), first + at, d, distances.index(d), at)))
             first += array.shape[0]
-    early, late = early[:-1], early[-1:]
     out = None
-    for part in (early, late):
+    for part in (items_all,):
         arrays, items = [], []
         for array, (count, first, d, source, at) in part:
             if not any(array is seen for seen in arrays):

time: 351 us -> 361 us (1.028)
  waiting for transfers between devices: 156 us -> 199 us
  starting transfers between devices: 71 us -> 42.7 us
  Pallas kernels: 117 us -> 112 us
    ppermute x45 -> x43, waiting for transfers between devices: 156 us -> 199 us  [permute(): return lax.ppermute(x, AXES, pairs)]
    ppermute x45 -> x43, starting transfers between devices: 71 us -> 42.7 us  [permute(): return lax.ppermute(x, AXES, pairs)]
    pallas_call x2 -> x1, Pallas kernels: 12.9 us -> 10.2 us  [write(): pl.pallas_call(functools.partial(write_kernel, items, len(stats), len(tot...]
    pallas_call x6 -> x5, Pallas kernels: 98.9 us -> 96.5 us  [the longest x3 92.4 us: logits_call(): pl.pallas_call(functools.partial(logits_kernel, n_blocks, n_groups, rows,...]
  transfers between devices with their start and end apart: 45 -> 43, of which waited for: 14 -> 18; matrix products, arithmetic and copies ran while one was open for 0% -> 0% of each run, Pallas kernels for 16% -> 15%
where the time goes in v2:
time: 361 us; the launch traced here: 360 us
  waiting for transfers between devices  199 us (55%)
  Pallas kernels  112 us (31%)
  starting transfers between devices  42.7 us (12%)
  local copies, waits for them, and re-layouts  5.42 us (2%)
    ppermute x43, waiting for transfers between devices, permute(): return lax.ppermute(x, AXES, pairs)  199 us
    pallas_call x3, Pallas kernels, logits_call(): pl.pallas_call(functools.partial(logits_kernel, n_blocks, n_groups, rows,...  92.4 us
    ppermute x43, starting transfers between devices, permute(): return lax.ppermute(x, AXES, pairs)  42.7 us
    pallas_call x1, Pallas kernels, write(): pl.pallas_call(functools.partial(write_kernel, items, len(stats), len(tot...  10.2 us
  transfers between devices with their start and end apart: 43, of which 18 were waited for; matrix products, arithmetic and copies ran while one was open for 0% of the time, Pallas kernels for 15%

profile of v2, /device:TPU:0, one launch (start us, length us, event | category | flops | bytes accessed | tf_op | source)
XLA Modules:
  0.0 359.5 jit_solution(621160507791583516)
XLA Ops:
  2.2 3.0 collective-permute-start.15
  6.7 2.6 collective-permute-start.2
  10.9 7.1 %collective-permute-done.15 = bf16[272,1024]{1,0:T(8,128)(2,1)S(1)} collective-permute-done((bf16[272,1024]{1,0:T(8,128)(2,1)}, bf16[272,1024]{1,0:T(8,128)(2,1)S(1)}, u32[]{:S(2)}, u32[]{:S(2)}) %collective-permute-start.15) | collective-permute-done | bytes 557088 | tf_op jit(solution)/shard_map/ppermute | solution.py:323
  18.1 2.8 collective-permute-start.18
  23.1 35.5 %collective-permute-done.2 = bf16[272,1024]{1,0:T(8,128)(2,1)S(1)} collective-permute-done((bf16[272,1024]{1,0:T(8,128)(2,1)}, bf16[272,1024]{1,0:T(8,128)(2,1)S(1)}, u32[]{:S(2)}, u32[]{:S(2)}) %collective-permute-start.2) | collective-permute-done | bytes 557088 | tf_op jit(solution)/shard_map/ppermute | solution.py:323
  60.7 9.9 %collective-permute-done.18 = bf16[272,1024]{1,0:T(8,128)(2,1)S(1)} collective-permute-done((bf16[272,1024]{1,0:T(8,128)(2,1)S(1)}, bf16[272,1024]{1,0:T(8,128)(2,1)S(1)}, u32[]{:S(2)}, u32[]{:S(2)}) %collective-permute-start.18) | collective-permute-done | bytes 557088 | tf_op jit(solution)/shard_map/ppermute | solution.py:323
  71.3 2.8 collective-permute-done.19
  74.6 8.4 %collective-permute-done.16 = bf16[272,1024]{1,0:T(8,128)(2,1)S(1)} collective-permute-done((bf16[272,1024]{1,0:T(8,128)(2,1)S(1)}, bf16[272,1024]{1,0:T(8,128)(2,1)S(1)}, u32[]{:S(2)}, u32[]{:S(2)}) %collective-permute-start.16) | collective-permute-done | bytes 557088 | tf_op jit(solution)/shard_map/ppermute | solution.py:323
  83.5 2.6 collective-permute-done.22
  86.6 11.4 %collective-permute-done.21 = bf16[272,1024]{1,0:T(8,128)(2,1)S(1)} collective-permute-done((bf16[272,1024]{1,0:T(8,128)(2,1)S(1)}, bf16[272,1024]{1,0:T(8,128)(2,1)S(1)}, u32[]{:S(2)}, u32[]{:S(2)}) %collective-permute-start.21) | collective-permute-done | bytes 557088 | tf_op jit(solution)/shard_map/ppermute | solution.py:323
  98.0 11.5 %collective-permute-done.20 = bf16[272,1024]{1,0:T(8,128)(2,1)S(1)} collective-permute-done((bf16[272,1024]{1,0:T(8,128)(2,1)S(1)}, bf16[272,1024]{1,0:T(8,128)(2,1)S(1)}, u32[]{:S(2)}, u32[]{:S(2)}) %collective-permute-start.20) | collective-permute-done | bytes 557088 | tf_op jit(solution)/shard_map/ppermute | solution.py:323
  110.0 14.3 %collective-permute-start.1 = (bf16[272,1024]{1,0:T(8,128)(2,1)}, bf16[272,1024]{1,0:T(8,128)(2,1)S(1)}, u32[]{:S(2)}, u32[]{:S(2)}) collective-permute-start(bf16[272,1024]{1,0:T(8,128)(2,1)} %shard_map.37.refs_16_.refs_3_), channel_id=1, source_target_pairs={{0,24},{1,25},{2,26},{3,27},{4,28},{5,29},{6,30},{7,31},{8,0},{9,1... | collective-permute-start | bytes 1671176 | tf_op jit(solution)/shard_map/ppermute | solution.py:323
  130.0 6.7 %collective-permute-done.1 = bf16[272,1024]{1,0:T(8,128)(2,1)S(1)} collective-permute-done((bf16[272,1024]{1,0:T(8,128)(2,1)}, bf16[272,1024]{1,0:T(8,128)(2,1)S(1)}, u32[]{:S(2)}, u32[]{:S(2)}) %collective-permute-start.1) | collective-permute-done | bytes 557088 | tf_op jit(solution)/shard_map/ppermute | solution.py:323
  137.2 18.2 %shard_map.39 = (bf16[1536,256]{1,0:T(8,128)(2,1)S(1)}, bf16[1536,256]{1,0:T(8,128)(2,1)S(1)}, f32[24,256]{1,0:T(8,128)S(1)}, f32[24,256]{1,0:T(8,128)S(1)}) custom-call(s32[1]{0:T(128)} %constant.0.clone.1.place_ref, bf16[4008,8192]{1,0:T(8,128)(2,1)} %bitcast.66, bf16[512,8192]{1,0:T(8,128)(2,1)S(1)} %get-tuple-element.21.refs_1_, ...), custom_call_target="tpu_custom_call" | custom-call | flops 12884901888 | bytes 33554432 | tf_op jit(solution)/shard_map/pallas_call | solution.py:199
  156.4 6.9 %collective-permute-done.5 = bf16[272,1024]{1,0:T(8,128)(2,1)S(1)} collective-permute-done((bf16[272,1024]{1,0:T(8,128)(2,1)S(1)}, bf16[272,1024]{1,0:T(8,128)(2,1)S(1)}, u32[]{:S(2)}, u32[]{:S(2)}) %collective-permute-start.5) | collective-permute-done | bytes 557088 | tf_op jit(solution)/shard_map/ppermute | solution.py:323
  163.8 29.4 %shard_map.40 = (bf16[2472,256]{1,0:T(8,128)(2,1)}, bf16[2472,256]{1,0:T(8,128)(2,1)S(1)}, f32[40,256]{1,0:T(8,128)S(1)}, f32[40,256]{1,0:T(8,128)S(1)}) custom-call(s32[1]{0:T(128)} %constant.0.clone.1.place_ref, bf16[4008,8192]{1,0:T(8,128)(2,1)} %bitcast.67, bf16[512,8192]{1,0:T(8,128)(2,1)S(1)} %get-tuple-element.21.refs_1_, ...), custom_call_target="tpu_custom_call" | custom-call | flops 20736638976 | bytes 48889856 | tf_op jit(solution)/shard_map/pallas_call | solution.py:199
  195.3 44.8 %shard_map.42 = (bf16[4008,256]{1,0:T(8,128)(2,1)S(1)}, bf16[4008,256]{1,0:T(8,128)(2,1)S(1)}, f32[64,256]{1,0:T(8,128)S(1)}, f32[64,256]{1,0:T(8,128)S(1)}) custom-call(s32[1]{0:T(128)} %constant.0.clone.1.place_ref, bf16[4008,8192]{1,0:T(8,128)(2,1)} %bitcast.68, bf16[512,8192]{1,0:T(8,128)(2,1)S(1)} %get-tuple-element.25.refs_1_, ...), custom_call_target="tpu_custom_call" | custom-call | flops 33621540864 | bytes 74055680 | tf_op jit(solution)/shard_map/pallas_call | solution.py:199
  245.6 55.9 %collective-permute-done.37.refs_2_.refs_8_ = f32[64,256]{1,0:T(8,128)S(1)} collective-permute-done((f32[64,256]{1,0:T(8,128)S(1)}, f32[64,256]{1,0:T(8,128)S(1)}, u32[]{:S(2)}, u32[]{:S(2)}) %collective-permute-start.37) | collective-permute-done | bytes 65568 | tf_op jit(solution)/shard_map/ppermute | solution.py:323
  305.5 3.4 collective-permute-done.39.refs_1_
  311.8 3.8 %collective-permute-done.42.refs_13_ = f32[8,256]{1,0:T(8,128)S(1)} collective-permute-done((f32[8,256]{1,0:T(8,128)}, f32[8,256]{1,0:T(8,128)S(1)}, u32[]{:S(2)}, u32[]{:S(2)}) %collective-permute-start.42) | collective-permute-done | bytes 8224 | tf_op jit(solution)/shard_map/ppermute | solution.py:323
  316.2 5.0 %collective-permute-done.40.refs_11_ = f32[8,256]{1,0:T(8,128)S(1)} collective-permute-done((f32[8,256]{1,0:T(8,128)}, f32[8,256]{1,0:T(8,128)S(1)}, u32[]{:S(2)}, u32[]{:S(2)}) %collective-permute-start.40) | collective-permute-done | bytes 8224 | tf_op jit(solution)/shard_map/ppermute | solution.py:323
  321.2 15.0 %collective-permute-done.32.refs_2_ = bf16[1536,256]{1,0:T(8,128)(2,1)S(1)} collective-permute-done((bf16[1536,256]{1,0:T(8,128)(2,1)}, bf16[1536,256]{1,0:T(8,128)(2,1)S(1)}, u32[]{:S(2)}, u32[]{:S(2)}) %collective-permute-start.32) | collective-permute-done | bytes 786464 | tf_op jit(solution)/shard_map/ppermute | solution.py:323
  336.3 11.9 %collective-permute-done.34.refs_4_ = bf16[1536,256]{1,0:T(8,128)(2,1)S(1)} collective-permute-done((bf16[1536,256]{1,0:T(8,128)(2,1)}, bf16[1536,256]{1,0:T(8,128)(2,1)S(1)}, u32[]{:S(2)}, u32[]{:S(2)}) %collective-permute-start.34) | collective-permute-done | bytes 786464 | tf_op jit(solution)/shard_map/ppermute | solution.py:323
  349.1 10.2 %shard_map.45 = f32[16032,256]{1,0:T(8,128)} custom-call(bf16[4008,256]{1,0:T(8,128)(2,1)} %copy-done.2, bf16[4008,256]{1,0:T(8,128)(2,1)} %collective-permute-done.31.refs_1_, bf16[1536,256]{1,0:T(8,128)(2,1)} %copy-done.6, bf16[2472,256]{1,0:T(8,128)(2,1)} %collective-permute-done.33.refs_3_, bf16[1536,256]{1,0:T(8,128)(2,1)} %copy-done.7, ...), custom_call_target="tpu_custom_call" | custom-call | bytes 24625152 | tf_op jit(solution)/shard_map/pallas_call | solution.py:291
  (104 shorter events, 36.0 us)
Async XLA Ops:
  6.7 51.9 %collective-permute-start.2 = (bf16[272,1024]{1,0:T(8,128)(2,1)}, bf16[272,1024]{1,0:T(8,128)(2,1)S(1)}, u32[]{:S(2)}, u32[]{:S(2)}) collective-permute-start(bf16[272,1024]{1,0:T(8,128)(2,1)} %shard_map.37.refs_16_.refs_3_), channel_id=1, source_target_pairs={{0,16},{1,17},{2,18},{3,19},{4,20},{5,21},{6,22},{7,23},{8,24},{9,... | collective-permute-start | bytes 1671176 | tf_op jit(solution)/shard_map/ppermute | solution.py:323
  9.3 49.8 %collective-permute-start = (bf16[272,1024]{1,0:T(8,128)(2,1)}, bf16[272,1024]{1,0:T(8,128)(2,1)S(1)}, u32[]{:S(2)}, u32[]{:S(2)}) collective-permute-start(bf16[272,1024]{1,0:T(8,128)(2,1)} %shard_map.37.refs_16_.refs_3_), channel_id=1, source_target_pairs={{0,8},{1,9},{2,10},{3,11},{4,12},{5,13},{6,14},{7,15},{8,16},{9,17... | collective-permute-start | bytes 1671176 | tf_op jit(solution)/shard_map/ppermute | solution.py:323
  18.1 52.5 %collective-permute-start.18 = (bf16[272,1024]{1,0:T(8,128)(2,1)S(1)}, bf16[272,1024]{1,0:T(8,128)(2,1)S(1)}, u32[]{:S(2)}, u32[]{:S(2)}) collective-permute-start(bf16[272,1024]{1,0:T(8,128)(2,1)S(1)} %collective-permute-done.15), channel_id=1, source_target_pairs={{0,16},{1,17},{2,18},{3,19},{4,20},{5,21},{6,22},{7,23},{8,24},{9,... | collective-permute-start | bytes 1671176 | tf_op jit(solution)/shard_map/ppermute | solution.py:323
  20.9 49.7 %collective-permute-start.23 = (bf16[272,1024]{1,0:T(8,128)(2,1)S(1)}, bf16[272,1024]{1,0:T(8,128)(2,1)S(1)}, u32[]{:S(2)}, u32[]{:S(2)}) collective-permute-start(bf16[272,1024]{1,0:T(8,128)(2,1)S(1)} %collective-permute-done.15), channel_id=1, source_target_pairs={{0,1},{1,0},{2,3},{3,2},{4,5},{5,4},{6,7},{7,6},{8,9},{9,8},{10,11... | collective-permute-start | bytes 1671176 | tf_op jit(solution)/shard_map/ppermute | solution.py:323
  20.9 50.2 %collective-permute-start.17 = (bf16[272,1024]{1,0:T(8,128)(2,1)S(1)}, bf16[272,1024]{1,0:T(8,128)(2,1)S(1)}, u32[]{:S(2)}, u32[]{:S(2)}) collective-permute-start(bf16[272,1024]{1,0:T(8,128)(2,1)S(1)} %collective-permute-done.15), channel_id=1, source_target_pairs={{0,24},{1,25},{2,26},{3,27},{4,28},{5,29},{6,30},{7,31},{8,0},{9,1... | collective-permute-start | bytes 1671176 | tf_op jit(solution)/shard_map/ppermute | solution.py:323
  83.0 26.5 %collective-permute-start.20 = (bf16[272,1024]{1,0:T(8,128)(2,1)S(1)}, bf16[272,1024]{1,0:T(8,128)(2,1)S(1)}, u32[]{:S(2)}, u32[]{:S(2)}) collective-permute-start(bf16[272,1024]{1,0:T(8,128)(2,1)S(1)} %collective-permute-done.16), channel_id=1, source_target_pairs={{0,4},{1,5},{2,6},{3,7},{4,0},{5,1},{6,2},{7,3},{8,12},{9,13},{10,... | collective-permute-start | bytes 1671176 | tf_op jit(solution)/shard_map/ppermute | solution.py:323
  86.1 38.2 %collective-permute-start.30 = (bf16[272,1024]{1,0:T(8,128)(2,1)S(1)}, bf16[272,1024]{1,0:T(8,128)(2,1)S(1)}, u32[]{:S(2)}, u32[]{:S(2)}) collective-permute-start(bf16[272,1024]{1,0:T(8,128)(2,1)S(1)} %collective-permute-done.22), channel_id=1, source_target_pairs={{0,1},{1,0},{2,3},{3,2},{4,5},{5,4},{6,7},{7,6},{8,9},{9,8},{10,11... | collective-permute-start | bytes 1671176 | tf_op jit(solution)/shard_map/ppermute | solution.py:323
  110.0 26.7 %collective-permute-start.1 = (bf16[272,1024]{1,0:T(8,128)(2,1)}, bf16[272,1024]{1,0:T(8,128)(2,1)S(1)}, u32[]{:S(2)}, u32[]{:S(2)}) collective-permute-start(bf16[272,1024]{1,0:T(8,128)(2,1)} %shard_map.37.refs_16_.refs_3_), channel_id=1, source_target_pairs={{0,24},{1,25},{2,26},{3,27},{4,28},{5,29},{6,30},{7,31},{8,0},{9,1... | collective-permute-start | bytes 1671176 | tf_op jit(solution)/shard_map/ppermute | solution.py:323
  124.3 31.2 %collective-permute-start.11 = (bf16[272,1024]{1,0:T(8,128)(2,1)S(1)}, bf16[272,1024]{1,0:T(8,128)(2,1)S(1)}, u32[]{:S(2)}, u32[]{:S(2)}) collective-permute-start(bf16[272,1024]{1,0:T(8,128)(2,1)S(1)} %collective-permute-done.3), channel_id=1, source_target_pairs={{0,1},{1,0},{2,3},{3,2},{4,5},{5,4},{6,7},{7,6},{8,9},{9,8},{10,11... | collective-permute-start | bytes 1671176 | tf_op jit(solution)/shard_map/ppermute | solution.py:323
  124.3 31.3 %collective-permute-start.10 = (bf16[272,1024]{1,0:T(8,128)(2,1)S(1)}, bf16[272,1024]{1,0:T(8,128)(2,1)S(1)}, u32[]{:S(2)}, u32[]{:S(2)}) collective-permute-start(bf16[272,1024]{1,0:T(8,128)(2,1)S(1)} %collective-permute-done.2), channel_id=1, source_target_pairs={{0,1},{1,0},{2,3},{3,2},{4,5},{5,4},{6,7},{7,6},{8,9},{9,8},{10,11... | collective-permute-start | bytes 1671176 | tf_op jit(solution)/shard_map/ppermute | solution.py:323
  124.8 31.2 %collective-permute-start.6 = (bf16[272,1024]{1,0:T(8,128)(2,1)S(1)}, bf16[272,1024]{1,0:T(8,128)(2,1)S(1)}, u32[]{:S(2)}, u32[]{:S(2)}) collective-permute-start(bf16[272,1024]{1,0:T(8,128)(2,1)S(1)} %collective-permute-done.2), channel_id=1, source_target_pairs={{0,4},{1,5},{2,6},{3,7},{4,0},{5,1},{6,2},{7,3},{8,12},{9,13},{10,... | collective-permute-start | bytes 1671176 | tf_op jit(solution)/shard_map/ppermute | solution.py:323
  128.4 34.9 %collective-permute-start.4 = (bf16[272,1024]{1,0:T(8,128)(2,1)S(1)}, bf16[272,1024]{1,0:T(8,128)(2,1)S(1)}, u32[]{:S(2)}, u32[]{:S(2)}) collective-permute-start(bf16[272,1024]{1,0:T(8,128)(2,1)S(1)} %collective-permute-done), channel_id=1, source_target_pairs={{0,4},{1,5},{2,6},{3,7},{4,0},{5,1},{6,2},{7,3},{8,12},{9,13},{10,... | collective-permute-start | bytes 1671176 | tf_op jit(solution)/shard_map/ppermute | solution.py:323
  136.7 26.6 %collective-permute-start.5 = (bf16[272,1024]{1,0:T(8,128)(2,1)S(1)}, bf16[272,1024]{1,0:T(8,128)(2,1)S(1)}, u32[]{:S(2)}, u32[]{:S(2)}) collective-permute-start(bf16[272,1024]{1,0:T(8,128)(2,1)S(1)} %collective-permute-done.1), channel_id=1, source_target_pairs={{0,4},{1,5},{2,6},{3,7},{4,0},{5,1},{6,2},{7,3},{8,12},{9,13},{10,... | collective-permute-start | bytes 1671176 | tf_op jit(solution)/shard_map/ppermute | solution.py:323
  155.5 37.7 %collective-permute-start.9 = (bf16[272,1024]{1,0:T(8,128)(2,1)S(1)}, bf16[272,1024]{1,0:T(8,128)(2,1)S(1)}, u32[]{:S(2)}, u32[]{:S(2)}) collective-permute-start(bf16[272,1024]{1,0:T(8,128)(2,1)S(1)} %collective-permute-done.1), channel_id=1, source_target_pairs={{0,1},{1,0},{2,3},{3,2},{4,5},{5,4},{6,7},{7,6},{8,9},{9,8},{10,11... | collective-permute-start | bytes 1671176 | tf_op jit(solution)/shard_map/ppermute | solution.py:323
  155.5 37.6 %collective-permute-start.8 = (bf16[272,1024]{1,0:T(8,128)(2,1)S(1)}, bf16[272,1024]{1,0:T(8,128)(2,1)S(1)}, u32[]{:S(2)}, u32[]{:S(2)}) collective-permute-start(bf16[272,1024]{1,0:T(8,128)(2,1)S(1)} %collective-permute-done), channel_id=1, source_target_pairs={{0,1},{1,0},{2,3},{3,2},{4,5},{5,4},{6,7},{7,6},{8,9},{9,8},{10,11... | collective-permute-start | bytes 1671176 | tf_op jit(solution)/shard_map/ppermute | solution.py:323
  156.0 37.1 %collective-permute-start.14 = (bf16[272,1024]{1,0:T(8,128)(2,1)S(1)}, bf16[272,1024]{1,0:T(8,128)(2,1)S(1)}, u32[]{:S(2)}, u32[]{:S(2)}) collective-permute-start(bf16[272,1024]{1,0:T(8,128)(2,1)S(1)} %collective-permute-done.6), channel_id=1, source_target_pairs={{0,1},{1,0},{2,3},{3,2},{4,5},{5,4},{6,7},{7,6},{8,9},{9,8},{10,11... | collective-permute-start | bytes 1671176 | tf_op jit(solution)/shard_map/ppermute | solution.py:323
  163.3 29.9 %collective-permute-start.13 = (bf16[272,1024]{1,0:T(8,128)(2,1)S(1)}, bf16[272,1024]{1,0:T(8,128)(2,1)S(1)}, u32[]{:S(2)}, u32[]{:S(2)}) collective-permute-start(bf16[272,1024]{1,0:T(8,128)(2,1)S(1)} %collective-permute-done.5), channel_id=1, source_target_pairs={{0,1},{1,0},{2,3},{3,2},{4,5},{5,4},{6,7},{7,6},{8,9},{9,8},{10,11... | collective-permute-start | bytes 1671176 | tf_op jit(solution)/shard_map/ppermute | solution.py:323
  163.3 29.9 %collective-permute-start.12 = (bf16[272,1024]{1,0:T(8,128)(2,1)S(1)}, bf16[272,1024]{1,0:T(8,128)(2,1)S(1)}, u32[]{:S(2)}, u32[]{:S(2)}) collective-permute-start(bf16[272,1024]{1,0:T(8,128)(2,1)S(1)} %collective-permute-done.4), channel_id=1, source_target_pairs={{0,1},{1,0},{2,3},{3,2},{4,5},{5,4},{6,7},{7,6},{8,9},{9,8},{10,11... | collective-permute-start | bytes 1671176 | tf_op jit(solution)/shard_map/ppermute | solution.py:323
  242.0 106.2 %collective-permute-start.31 = (bf16[4008,256]{1,0:T(8,128)(2,1)S(1)}, bf16[4008,256]{1,0:T(8,128)(2,1)}, u32[]{:S(2)}, u32[]{:S(2)}) collective-permute-start(bf16[4008,256]{1,0:T(8,128)(2,1)S(1)} %get-tuple-element.28), channel_id=1, source_target_pairs={{0,1},{1,0},{2,3},{3,2},{4,5},{5,4},{6,7},{7,6},{8,9},{9,8},{10,11... | collective-permute-start | bytes 6156296 | tf_op jit(solution)/shard_map/ppermute | solution.py:323
  242.1 106.1 %collective-permute-start.33 = (bf16[2472,256]{1,0:T(8,128)(2,1)}, bf16[2472,256]{1,0:T(8,128)(2,1)}, u32[]{:S(2)}, u32[]{:S(2)}) collective-permute-start(bf16[2472,256]{1,0:T(8,128)(2,1)} %get-tuple-element.30), channel_id=1, source_target_pairs={{0,2},{1,3},{2,0},{3,1},{4,6},{5,7},{6,4},{7,5},{8,10},{9,11},{10,... | collective-permute-start | bytes 3797000 | tf_op jit(solution)/shard_map/ppermute | solution.py:323
  242.6 105.6 %collective-permute-start.35 = (bf16[2472,256]{1,0:T(8,128)(2,1)S(1)}, bf16[2472,256]{1,0:T(8,128)(2,1)}, u32[]{:S(2)}, u32[]{:S(2)}) collective-permute-start(bf16[2472,256]{1,0:T(8,128)(2,1)S(1)} %get-tuple-element.32), channel_id=1, source_target_pairs={{0,3},{1,2},{2,1},{3,0},{4,7},{5,6},{6,5},{7,4},{8,11},{9,10},{10,... | collective-permute-start | bytes 3797000 | tf_op jit(solution)/shard_map/ppermute | solution.py:323
  243.9 57.6 %collective-permute-start.37 = (f32[64,256]{1,0:T(8,128)S(1)}, f32[64,256]{1,0:T(8,128)S(1)}, u32[]{:S(2)}, u32[]{:S(2)}) collective-permute-start(f32[64,256]{1,0:T(8,128)S(1)} %pad_maximum_fusion), channel_id=1, source_target_pairs={{0,2},{1,3},{2,0},{3,1},{4,6},{5,7},{6,4},{7,5},{8,10},{9,11},{10,... | collective-permute-start | bytes 196616 | tf_op jit(solution)/shard_map/ppermute | solution.py:323
  244.5 57.5 %collective-permute-start.38 = (f32[64,256]{1,0:T(8,128)S(1)}, f32[64,256]{1,0:T(8,128)S(1)}, u32[]{:S(2)}, u32[]{:S(2)}) collective-permute-start(f32[64,256]{1,0:T(8,128)S(1)} %pad_maximum_fusion.1), channel_id=1, source_target_pairs={{0,3},{1,2},{2,1},{3,0},{4,7},{5,6},{6,5},{7,4},{8,11},{9,10},{10,... | collective-permute-start | bytes 196616 | tf_op jit(solution)/shard_map/ppermute | solution.py:323
  321.2 27.0 %collective-permute-start.34 = (bf16[1536,256]{1,0:T(8,128)(2,1)}, bf16[1536,256]{1,0:T(8,128)(2,1)S(1)}, u32[]{:S(2)}, u32[]{:S(2)}) collective-permute-start(bf16[1536,256]{1,0:T(8,128)(2,1)} %copy-done.4), channel_id=1, source_target_pairs={{0,3},{1,2},{2,1},{3,0},{4,7},{5,6},{6,5},{7,4},{8,11},{9,10},{10,... | collective-permute-start | bytes 2359304 | tf_op jit(solution)/shard_map/ppermute | solution.py:323
  (34 other events, 453.1 us)
